TPU v7x, 32 devices: a whole 2x2x4 slice. The times are simulated.
32 devices in a mesh: comp: 2 (over core), tgt: 4 (over y, x), src: 4 (over z).
Axes of the slice: x: 2, y: 2, z: 4, core: 2. Of those that a mesh axis runs over, the one named last changes fastest.
Arguments:
- field: bfloat16 [3, 32, 8192], P(None, None, ('tgt', 'src')), may hold values from -6 to 6
- dest_group: int32 [4096, 1], P(('comp', 'tgt', 'src')), may hold values from 0 to 3; in each aligned block of 128 rows (0 to 127, 128 to 255, ...) at most 64 rows name the same one
- src_local: int32 [4096], P(('comp', 'tgt', 'src')), may hold values from 0 to 1
- ranks: int32 [4096], P(('comp', 'tgt', 'src')), may hold values from 8 to 64
- mixing: float32 [4096, 3, 3], P(('comp', 'tgt', 'src')), may hold values from -5 to 5
- v_factor: bfloat16 [4096, 64, 256], P(('comp', 'tgt', 'src')), may hold values from -0.375 to 0.375
- u_factor: bfloat16 [8192, 64, 256], P(('comp', 'tgt', 'src')), may hold values from -0.0625 to 0.0625
- slot_cluster: int32 [8192], P(('comp', 'tgt', 'src')), may hold values from 0 to 7
- near_src: int32 [128], P(('comp', 'tgt', 'src')), may hold values from 0 to 1
- near_tgt: int32 [128], P(('comp', 'tgt', 'src')), may hold values from 0 to 7
- near_mixing: float32 [128, 3, 3], P(('comp', 'tgt', 'src')), may hold values from -5 to 5
- near_matrix: bfloat16 [128, 256, 256], P(('comp', 'tgt', 'src')), may hold values from -0.1875 to 0.1875
Outputs:
- result: float32 [3, 32, 8192], P(None, None, ('comp', 'tgt', 'src'))
Inputs may be any that keep to these rules, and one draw needn't show every extreme that they name: `dest_group`: among the 128 blocks of one device at most 64 name the same target group, and in every draw some device has exactly 64 blocks to one group.
All inputs are finite; a program needn't handle non-finite values.
Results may differ from a plain program's by a relative error of at most 0.0018.
Values may be sent and summed in bfloat16 or wider, within the bound.
A program may use at most 128 MiB of HBM per device.

v0:
```python
import functools

import jax
import jax.numpy as jnp
from jax import lax
from jax.experimental import pallas as pl
from jax.experimental.pallas import tpu as pltpu
from jax.sharding import PartitionSpec as P

NT = (((1,), (1,)), ((), ()))
MESH = pl.DeviceIdType.MESH
HALVES = 2


def mix_rows(weights, parts):
    mixed = []
    for row in weights:
        total = row[0] * parts[0]
        for weight, part in zip(row[1:], parts[1:]):
            total = total + weight * part
        mixed.append(total)
    return mixed


def fused_kernel(
    sizes,
    field_hbm,
    dest_hbm,
    src_hbm,
    ranks_hbm,
    mix_ref,
    v_hbm,
    u_hbm,
    cluster,
    near_src,
    near_tgt,
    near_mix,
    near_hbm,
    out_ref,
    field_ref,
    x_ref,
    v_ref,
    u_ref,
    near_ref,
    rows_ref,
    meta_ref,
    meta,
    near_out,
    sent,
    got,
    lhs,
    acc,
    comp_got,
    total,
    cast,
    src_got,
    load_sem,
    u_sem,
    meta_sem,
    send_sem,
    recv_sem,
    comp_send,
    comp_recv,
    src_send,
    src_recv,
):
    groups, shards, pairing, components, chunk = sizes
    me = lax.axis_index("tgt")
    row = lax.axis_index("src")
    half_of = lax.axis_index("comp")
    owned, channels, size = x_ref.shape
    vectors = channels // components
    strip = vectors // HALVES
    band = components * strip
    slots, rank_width = u_hbm.shape[0] * 2, u_hbm.shape[1] // 2
    blocks = v_hbm.shape[0]
    capacity = slots // groups
    pairs = capacity // 2
    lanes = 2 * rank_width
    chunks = pairs // chunk
    targets = acc.shape[1] // band
    kept = targets // (pairing * shards)

    def load(index, source, target):
        return pltpu.make_async_copy(source, target, load_sem.at[index])

    small = [
        load(0, dest_hbm, rows_ref.at[0]),
        load(1, ranks_hbm, rows_ref.at[1]),
        load(2, src_hbm, rows_ref.at[2]),
    ]
    large = [load(3, field_hbm, field_ref), load(4, near_hbm, near_ref)]
    split = 4 if blocks % 4 == 0 else 1
    part = blocks // split
    v_loads = [
        load(5 + i, v_hbm.at[pl.ds(i * part, part)], v_ref.at[pl.ds(i * part, part)])
        for i in range(split)
    ]
    u_loads = [
        pltpu.make_async_copy(
            u_hbm.at[pl.ds(g * pairs, pairs)], u_ref.at[pl.ds(g * pairs, pairs)], u_sem.at[g]
        )
        for g in range(groups)
    ]
    for copy in small + large[:1] + v_loads + large[1:] + u_loads:
        copy.start()

    barrier = pltpu.get_barrier_semaphore()
    for step in range(1, groups):
        pl.semaphore_signal(
            barrier, inc=1, device_id={"tgt": jnp.bitwise_xor(me, step)}, device_id_type=MESH
        )
    for step in range(1, shards):
        pl.semaphore_signal(
            barrier, inc=1, device_id={"src": lax.rem(row + step, shards)}, device_id_type=MESH
        )
    for step in range(1, pairing):
        pl.semaphore_signal(
            barrier, inc=1, device_id={"comp": lax.rem(half_of + step, pairing)}, device_id_type=MESH
        )

    for copy in small:
        copy.wait()
    dest = rows_ref[0]
    padded = -(-groups // 16) * 16
    member = jnp.where(
        lax.broadcasted_iota(jnp.int32, (padded, blocks), 0) == dest, 1.0, 0.0
    )
    before = jnp.where(
        lax.broadcasted_iota(jnp.int32, (blocks, blocks), 0)
        < lax.broadcasted_iota(jnp.int32, (blocks, blocks), 1),
        1.0,
        0.0,
    ).astype(jnp.bfloat16)
    earlier = jnp.dot(member.astype(jnp.bfloat16), before, preferred_element_type=jnp.float32)
    position = jnp.sum(member * earlier, axis=0, keepdims=True)
    slot = dest * capacity + position.astype(jnp.int32)
    taken = jnp.where(
        lax.broadcasted_iota(jnp.int32, (slots, blocks), 0) == slot, 1.0, 0.0
    ).astype(jnp.bfloat16)
    line = lax.broadcasted_iota(jnp.int32, (16, blocks), 0)
    facts = jnp.where(
        line == 0,
        lax.broadcasted_iota(jnp.int32, (16, blocks), 1),
        jnp.where(line == 1, rows_ref[1], rows_ref[2]),
    )
    placed = lax.dot_general(
        facts.astype(jnp.float32).astype(jnp.bfloat16), taken, NT, preferred_element_type=jnp.float32
    )
    meta_ref[...] = placed[:8].astype(jnp.int32)
    to_scalars = pltpu.make_async_copy(meta_ref, meta, meta_sem)
    to_scalars.start()

    large[0].wait()
    for s in range(owned):
        x_ref[s] = field_ref[:, s * size : (s + 1) * size]
    to_scalars.wait()
    for copy in v_loads:
        copy.wait()

    lane = lax.broadcasted_iota(jnp.int32, (1, lanes), 1)
    first = lane < rank_width
    rank_at = lane % rank_width
    unroll = 4 if chunk % 4 == 0 else 1

    def coef_step(offset, start):
        base = jnp.bitwise_xor(me, offset) * capacity + 2 * start
        numbers = [jnp.clip(meta[0, base + i], 0, blocks - 1) for i in range(2 * unroll)]
        v = jnp.concatenate([v_ref[b] for b in numbers], axis=0)
        x = x_ref[...].reshape(owned * channels, size)
        y = lax.dot_general(x, v, NT, preferred_element_type=jnp.float32)
        for u in range(unroll):
            b0, b1 = numbers[2 * u], numbers[2 * u + 1]
            k0, k1 = base + 2 * u, base + 2 * u + 1
            here = y[:, u * lanes : (u + 1) * lanes]
            chosen = jnp.where(first, meta[2, k0], meta[2, k1])
            coef = here[:channels]
            for s in range(1, owned):
                coef = jnp.where(chosen == s, here[s * channels : (s + 1) * channels], coef)
            coef = jnp.where(rank_at < jnp.where(first, meta[1, k0], meta[1, k1]), coef, 0.0)
            weights = [
                [jnp.where(first, mix_ref[c, d, b0], mix_ref[c, d, b1]) for d in range(components)]
                for c in range(components)
            ]
            mixed = mix_rows(
                weights, [coef[d * vectors : (d + 1) * vectors] for d in range(components)]
            )
            for h in range(HALVES):
                for c in range(components):
                    sent[offset, h, start + u, c * strip : (c + 1) * strip, :] = mixed[c][
                        h * strip : (h + 1) * strip
                    ].astype(jnp.bfloat16)

    def coef_chunk(offset, c):
        def several(step, carry):
            coef_step(offset, c * chunk + step * unroll)
            return carry

        lax.fori_loop(0, chunk // unroll, several, 0)

    def exchange(offset, h, c):
        where = (h, pl.ds(c * chunk, chunk))
        return pltpu.make_async_remote_copy(
            src_ref=sent.at[(offset,) + where],
            dst_ref=got.at[(offset - 1,) + where],
            send_sem=send_sem.at[h, offset - 1, c],
            recv_sem=recv_sem.at[h, offset - 1, c],
            device_id={"tgt": jnp.bitwise_xor(me, offset)},
            device_id_type=MESH,
        )

    def over_offsets(action):
        def step(t, carry):
            action(groups - 1 - t)
            return carry

        lax.fori_loop(0, groups - 1, step, 0)

    def over_chunks(action):
        def step(c, carry):
            action(c)
            return carry

        lax.fori_loop(0, chunks, step, 0)

    pl.semaphore_wait(barrier, groups + shards + pairing - 3)

    def send_first(c):
        def one(offset):
            coef_chunk(offset, c)
            exchange(offset, 0, c).start()

        over_offsets(one)

    over_chunks(send_first)
    for h in range(1, HALVES):
        over_chunks(lambda c, h=h: over_offsets(lambda offset: exchange(offset, h, c).start()))
    over_chunks(lambda c: coef_chunk(0, c))

    large[1].wait()
    for n in range(near_ref.shape[0]):
        y = lax.dot_general(
            x_ref[near_src[n]], near_ref[n], NT, preferred_element_type=jnp.float32
        )
        weights = [[near_mix[c, n, d] for d in range(components)] for c in range(components)]
        mixed = mix_rows(weights, [y[d * vectors : (d + 1) * vectors] for d in range(components)])
        for h in range(HALVES):
            for c in range(components):
                near_out[h, n, c * strip : (c + 1) * strip, :] = mixed[c][
                    h * strip : (h + 1) * strip
                ]

    def place_near(w, carry):
        for h in range(HALVES):
            value = jnp.where(near_tgt[0] == w, near_out[h, 0], 0.0)
            for n in range(1, near_ref.shape[0]):
                value = value + jnp.where(near_tgt[n] == w, near_out[h, n], 0.0)
            acc[h, pl.ds(pl.multiple_of(w * band, band), band), :] = value
        return carry

    lax.fori_loop(0, targets, place_near, 0)
    for copy in u_loads:
        copy.wait()

    wide_first = lax.broadcasted_iota(jnp.int32, (strip, lanes), 1) < rank_width

    def far(h, offset, c, read):
        base = jnp.bitwise_xor(me, offset) * pairs + c * chunk
        for u in range(chunk):
            ids = jnp.where(wide_first, cluster[2 * (base + u)], cluster[2 * (base + u) + 1])
            value = read(c * chunk + u)
            for w in range(targets):
                on = jnp.where(ids == w, 1.0, 0.0).astype(jnp.bfloat16)
                for c3 in range(components):
                    lhs[pl.ds(w * band + c3 * strip, strip), u * lanes : (u + 1) * lanes] = (
                        value[c3 * strip : (c3 + 1) * strip] * on
                    )
        basis = u_ref[pl.ds(base, chunk)].reshape(chunk * lanes, size)
        acc[h] += jnp.dot(lhs[...], basis, preferred_element_type=jnp.float32)

    def far_own(h):
        over_chunks(lambda c: far(h, 0, c, lambda m: sent[0, h, m]))

    def far_chunk(h, c):
        def one(offset):
            exchange(offset, h, c).wait_recv()
            far(h, offset, c, lambda m: got[offset - 1, h, m])

        over_offsets(one)

    portion = shards * kept * band

    def comp_copy(h, step):
        to = lax.rem(half_of + step, pairing)
        return pltpu.make_async_remote_copy(
            src_ref=acc.at[h, pl.ds(pl.multiple_of(to * portion, portion), portion)],
            dst_ref=comp_got.at[h, step - 1],
            send_sem=comp_send.at[h, step - 1],
            recv_sem=comp_recv.at[h, step - 1],
            device_id={"comp": to},
            device_id_type=MESH,
        )

    piece = kept * band

    def src_copy(h, step):
        to = lax.rem(row + step, shards)
        return pltpu.make_async_remote_copy(
            src_ref=cast.at[h, pl.ds(pl.multiple_of(to * piece, piece), piece)],
            dst_ref=src_got.at[h, step - 1],
            send_sem=src_send.at[h, step - 1],
            recv_sem=src_recv.at[h, step - 1],
            device_id={"src": to},
            device_id_type=MESH,
        )

    def share_comp(h):
        for step in range(1, pairing):
            comp_copy(h, step).start()

    def share_src(h):
        for step in range(1, pairing):
            comp_copy(h, step).wait_recv()
        value = acc[h, pl.ds(pl.multiple_of(half_of * portion, portion), portion), :]
        for step in range(1, pairing):
            value = value + comp_got[h, step - 1]
        total[h] = value
        cast[h] = value.astype(jnp.bfloat16)
        for step in range(1, shards):
            src_copy(h, step).start()

    def finish(h):
        value = total[h, pl.ds(pl.multiple_of(row * piece, piece), piece), :]
        for step in range(1, shards):
            src_copy(h, step).wait_recv()
            value = value + src_got[h, step - 1].astype(jnp.float32)
        for k in range(kept):
            for c in range(components):
                at = k * band + c * strip
                out_ref[c, h * strip : (h + 1) * strip, k * size : (k + 1) * size] = value[
                    at : at + strip
                ]

    for h in range(HALVES):
        far_own(h)
    for h in range(HALVES):
        over_chunks(functools.partial(far_chunk, h))
        share_comp(h)
        share_src(h)
        if h:
            finish(h - 1)
    finish(HALVES - 1)

    for h in range(HALVES):
        over_chunks(lambda c, h=h: over_offsets(lambda offset: exchange(offset, h, c).wait_send()))
        for step in range(1, pairing):
            comp_copy(h, step).wait_send()
        for step in range(1, shards):
            src_copy(h, step).wait_send()


def body(
    field,
    dest_group,
    src_local,
    ranks,
    mixing,
    v_factor,
    u_factor,
    slot_cluster,
    near_src,
    near_tgt,
    near_mixing,
    near_matrix,
):
    groups = lax.axis_size("tgt")
    shards = lax.axis_size("src")
    pairing = lax.axis_size("comp")
    blocks, rank_width, size = v_factor.shape
    components, vectors, points = field.shape
    channels = components * vectors
    owned = points // size
    slots = u_factor.shape[0]
    pairs = slots // groups // 2
    targets = owned * shards
    kept = targets // (pairing * shards)
    lanes = 2 * rank_width
    chunk = 8 if pairs % 8 == 0 else pairs
    chunks = pairs // chunk
    band = channels // HALVES
    near_count = near_matrix.shape[0]
    smem = pl.BlockSpec(memory_space=pltpu.SMEM)
    anywhere = pl.BlockSpec(memory_space=pl.ANY)
    f32, bf16, i32 = jnp.float32, jnp.bfloat16, jnp.int32
    dma = pltpu.SemaphoreType.DMA
    return pl.pallas_call(
        functools.partial(fused_kernel, (groups, shards, pairing, components, chunk)),
        out_shape=jax.ShapeDtypeStruct((components, vectors, kept * size), f32),
        in_specs=[anywhere] * 4 + [smem] + [anywhere] * 2 + [smem] * 4 + [anywhere],
        out_specs=pl.BlockSpec(memory_space=pltpu.VMEM),
        scratch_shapes=[
            pltpu.VMEM((channels, points), bf16),
            pltpu.VMEM((owned, channels, size), bf16),
            pltpu.VMEM((blocks, rank_width, size), bf16),
            pltpu.VMEM((slots // 2, lanes, size), bf16),
            pltpu.VMEM((near_count, size, size), bf16),
            pltpu.VMEM((3, 1, blocks), i32),
            pltpu.VMEM((8, slots), i32),
            pltpu.SMEM((8, slots), i32),
            pltpu.VMEM((HALVES, near_count, band, size), f32),
            pltpu.VMEM((groups, HALVES, pairs, band, lanes), bf16),
            pltpu.VMEM((groups - 1, HALVES, pairs, band, lanes), bf16),
            pltpu.VMEM((targets * band, chunk * lanes), bf16),
            pltpu.VMEM((HALVES, targets * band, size), f32),
            pltpu.VMEM((HALVES, pairing - 1, shards * kept * band, size), f32),
            pltpu.VMEM((HALVES, shards * kept * band, size), f32),
            pltpu.VMEM((HALVES, shards * kept * band, size), bf16),
            pltpu.VMEM((HALVES, shards - 1, kept * band, size), bf16),
            dma((9,)),
            dma((groups,)),
            dma,
            dma((HALVES, groups - 1, chunks)),
            dma((HALVES, groups - 1, chunks)),
            dma((HALVES, pairing - 1)),
            dma((HALVES, pairing - 1)),
            dma((HALVES, shards - 1)),
            dma((HALVES, shards - 1)),
        ],
        compiler_params=pltpu.CompilerParams(collective_id=0, has_side_effects=True),
        name="fused",
    )(
        field.reshape(channels, points),
        dest_group.reshape(1, -1),
        src_local.reshape(1, -1),
        ranks.reshape(1, -1),
        mixing.transpose(1, 2, 0),
        v_factor,
        u_factor.reshape(slots // 2, lanes, size),
        slot_cluster,
        near_src,
        near_tgt,
        near_mixing.transpose(1, 0, 2),
        near_matrix,
    )


def solution(mesh):
    everywhere = ("comp", "tgt", "src")
    placed = (
        P(None, None, ("tgt", "src")),
        P(everywhere, None),
        P(everywhere),
        P(everywhere),
        P(everywhere, None, None),
        P(everywhere, None, None),
        P(everywhere, None, None),
        P(everywhere),
        P(everywhere),
        P(everywhere),
        P(everywhere, None, None),
        P(everywhere, None, None),
    )
    return jax.shard_map(
        body,
        mesh=mesh,
        in_specs=placed,
        out_specs=P(None, None, everywhere),
        check_vma=False,
    )
```

profile of v0, /device:TPU:0, one launch (start us, length us, event | category | flops | bytes accessed | tf_op | source)
XLA Modules:
  0.0 53.0 jit_solution(4711780733305961367)
XLA Ops:
  0.0 51.5 %fused.1 = f32[3,32,256]{2,1,0:T(8,128)} custom-call(bf16[96,512]{1,0:T(8,128)(2,1)} %bitcast.8, s32[1,128]{1,0:T(1,128)} %bitcast.11, s32[1,128]{1,0:T(1,128)} %bitcast.12, s32[1,128]{1,0:T(1,128)} %bitcast.13, f32[3,3,128]{2,1,0:T(4,128)} %bitcast.9, bf16[128,64,256]{2,1,0:T(8,128)(2,1)} %v_hbm.1, bf16[128,128,256]{2,1,0:T(8,128)(2,1)} %bitcast.7, ...), custom_call_target="tpu_custom_call" | custom-call | tf_op jit(solution)/shard_map/fused/pallas_call | solution.py:396
  51.5 1.5 %copy.14 = f32[3,32,256]{2,1,0:T(8,128)} copy(f32[3,32,256]{2,1,0:T(8,128)} %fused.1) | data formatting | bytes 196608
where the time goes:
time: 53.2 us; the launch traced here: 53 us
  Pallas kernels  51.5 us (97%)
  local copies, waits for them, and re-layouts  1.54 us (3%)
    pallas_call x1, Pallas kernels, body(): pl.pallas_call(functools.partial(fused_kernel, (groups, shards, pairing,...  51.5 us
    unnamed x1, local copies, waits for them, and re-layouts  1.54 us

commit v1 on v0

--- a/solution.py
+++ b/solution.py
@@ -1,4 +1,5 @@
 import functools
+import math
 
 import jax
 import jax.numpy as jnp
@@ -10,6 +11,18 @@
 NT = (((1,), (1,)), ((), ()))
 MESH = pl.DeviceIdType.MESH
 HALVES = 2
+TILE = 16
+TILE_BITS = 4
+
+
+def cut(length):
+    plan, begin = [], 0
+    while begin < length:
+        left = length - begin
+        size = 8 if left > 12 else min(left, max(4, left - 4))
+        plan.append((begin, size))
+        begin += size
+    return tuple(plan)
 
 
 def mix_rows(weights, parts):
@@ -28,13 +41,13 @@
     dest_hbm,
     src_hbm,
     ranks_hbm,
-    mix_ref,
+    mix_hbm,
     v_hbm,
     u_hbm,
-    cluster,
-    near_src,
-    near_tgt,
-    near_mix,
+    cluster_hbm,
+    near_src_hbm,
+    near_tgt_hbm,
+    near_mix_hbm,
     near_hbm,
     out_ref,
     field_ref,
@@ -45,6 +58,11 @@
     rows_ref,
     meta_ref,
     meta,
+    mix_ref,
+    cluster,
+    near_src,
+    near_tgt,
+    near_mix,
     near_out,
     sent,
     got,
@@ -89,7 +107,14 @@
         load(1, ranks_hbm, rows_ref.at[1]),
         load(2, src_hbm, rows_ref.at[2]),
     ]
-    large = [load(3, field_hbm, field_ref), load(4, near_hbm, near_ref)]
+    early = [load(3, field_hbm, field_ref), load(4, mix_hbm, mix_ref)]
+    later = [
+        load(9, near_hbm, near_ref),
+        load(10, cluster_hbm, cluster),
+        load(11, near_src_hbm, near_src),
+        load(12, near_tgt_hbm, near_tgt),
+        load(13, near_mix_hbm, near_mix),
+    ]
     split = 4 if blocks % 4 == 0 else 1
     part = blocks // split
     v_loads = [
@@ -102,7 +127,7 @@
         )
         for g in range(groups)
     ]
-    for copy in small + large[:1] + v_loads + large[1:] + u_loads:
+    for copy in small + early + v_loads:
         copy.start()
 
     barrier = pltpu.get_barrier_semaphore()
@@ -151,12 +176,14 @@
     to_scalars = pltpu.make_async_copy(meta_ref, meta, meta_sem)
     to_scalars.start()
 
-    large[0].wait()
+    early[0].wait()
     for s in range(owned):
         x_ref[s] = field_ref[:, s * size : (s + 1) * size]
     to_scalars.wait()
-    for copy in v_loads:
+    for copy in early[1:] + v_loads:
         copy.wait()
+    for copy in later + u_loads:
+        copy.start()
 
     lane = lax.broadcasted_iota(jnp.int32, (1, lanes), 1)
     first = lane < rank_width
@@ -237,7 +264,8 @@
         over_chunks(lambda c, h=h: over_offsets(lambda offset: exchange(offset, h, c).start()))
     over_chunks(lambda c: coef_chunk(0, c))
 
-    large[1].wait()
+    for copy in later:
+        copy.wait()
     for n in range(near_ref.shape[0]):
         y = lax.dot_general(
             x_ref[near_src[n]], near_ref[n], NT, preferred_element_type=jnp.float32
@@ -353,6 +381,485 @@
 
     for h in range(HALVES):
         over_chunks(lambda c, h=h: over_offsets(lambda offset: exchange(offset, h, c).wait_send()))
+        for step in range(1, pairing):
+            comp_copy(h, step).wait_send()
+        for step in range(1, shards):
+            src_copy(h, step).wait_send()
+
+
+def packed_kernel(
+    sizes,
+    field_hbm,
+    dest_hbm,
+    src_hbm,
+    ranks_hbm,
+    mix_hbm,
+    v_hbm,
+    u_hbm,
+    cluster_hbm,
+    near_src_hbm,
+    near_tgt_hbm,
+    near_mix_hbm,
+    near_hbm,
+    out_ref,
+    flag_ref,
+    field_ref,
+    x_ref,
+    v_ref,
+    u_ref,
+    near_ref,
+    rows_ref,
+    meta_ref,
+    meta,
+    mix_ref,
+    weight_ref,
+    table_got,
+    table,
+    flag_row,
+    flag_got,
+    cluster,
+    near_src,
+    near_tgt,
+    near_mix,
+    near_out,
+    sent,
+    got,
+    lhs,
+    rhs,
+    acc,
+    comp_got,
+    total,
+    cast,
+    src_got,
+    load_sem,
+    u_sem,
+    meta_sem,
+    send_sem,
+    recv_sem,
+    comp_send,
+    comp_recv,
+    src_send,
+    src_recv,
+    table_send,
+    table_recv,
+    table_sem,
+    flag_send,
+    flag_recv,
+):
+    groups, shards, pairing, components, limit, plan = sizes
+    me = lax.axis_index("tgt")
+    row = lax.axis_index("src")
+    half_of = lax.axis_index("comp")
+    owned, channels, size = x_ref.shape
+    vectors = channels // components
+    strip = vectors // HALVES
+    band = components * strip
+    lanes = sent.shape[-1]
+    tiles_in = lanes // TILE
+    whole = sent.shape[2]
+    full = whole * tiles_in
+    blocks = weight_ref.shape[0]
+    tiles = v_hbm.shape[0]
+    per_block = tiles // blocks
+    capacity = full // per_block
+    targets = acc.shape[1] // band
+    kept = targets // (pairing * shards)
+
+    def load(index, source, target):
+        return pltpu.make_async_copy(source, target, load_sem.at[index])
+
+    small = [
+        load(0, dest_hbm, rows_ref.at[0]),
+        load(1, ranks_hbm, rows_ref.at[1]),
+        load(2, src_hbm, rows_ref.at[2]),
+    ]
+    early = [load(3, field_hbm, field_ref), load(4, mix_hbm, mix_ref)]
+    later = [
+        load(9, near_hbm, near_ref),
+        load(10, cluster_hbm, cluster),
+        load(11, near_src_hbm, near_src),
+        load(12, near_tgt_hbm, near_tgt),
+        load(13, near_mix_hbm, near_mix),
+    ]
+    split = 4 if tiles % 4 == 0 else 1
+    part = tiles // split
+    v_loads = [
+        load(5 + i, v_hbm.at[pl.ds(i * part, part)], v_ref.at[pl.ds(i * part, part)])
+        for i in range(split)
+    ]
+    u_loads = [
+        pltpu.make_async_copy(
+            u_hbm.at[pl.ds(g * full, full)], u_ref.at[pl.ds(g * full, full)], u_sem.at[g]
+        )
+        for g in range(groups)
+    ]
+    for copy in small + early + v_loads:
+        copy.start()
+
+    barrier = pltpu.get_barrier_semaphore()
+    for step in range(1, groups):
+        pl.semaphore_signal(
+            barrier, inc=1, device_id={"tgt": jnp.bitwise_xor(me, step)}, device_id_type=MESH
+        )
+    for step in range(1, shards):
+        pl.semaphore_signal(
+            barrier, inc=1, device_id={"src": lax.rem(row + step, shards)}, device_id_type=MESH
+        )
+    for step in range(1, pairing):
+        pl.semaphore_signal(
+            barrier, inc=1, device_id={"comp": lax.rem(half_of + step, pairing)}, device_id_type=MESH
+        )
+
+    for copy in small:
+        copy.wait()
+    dest, rank, source = rows_ref[0], rows_ref[1], rows_ref[2]
+    count = lax.shift_right_logical(rank + (TILE - 1), TILE_BITS)
+    padded = -(-groups // 16) * 16
+    group_at = lax.broadcasted_iota(jnp.int32, (padded, blocks), 0)
+    member = jnp.where(group_at == dest, 1.0, 0.0)
+    both = jnp.concatenate([member, member * count.astype(jnp.float32)], axis=0)
+    before = jnp.where(
+        lax.broadcasted_iota(jnp.int32, (blocks, blocks), 0)
+        < lax.broadcasted_iota(jnp.int32, (blocks, blocks), 1),
+        1.0,
+        0.0,
+    ).astype(jnp.bfloat16)
+    earlier = jnp.dot(both.astype(jnp.bfloat16), before, preferred_element_type=jnp.float32)
+    position = jnp.sum(member * earlier[:padded], axis=0, keepdims=True).astype(jnp.int32)
+    tile_at = jnp.sum(member * earlier[padded:], axis=0, keepdims=True).astype(jnp.int32)
+    used = jnp.sum(both[padded:], axis=1, keepdims=True)
+    away = lax.broadcasted_iota(jnp.int32, (padded, 1), 0) != me
+    most = jnp.max(jnp.where(away, used, 0.0), axis=0, keepdims=True)
+    over = jnp.where(most > float(limit * tiles_in), 1, 0)
+    start = dest * full + tile_at
+    ahead = lax.broadcasted_iota(jnp.int32, (groups * full, blocks), 0) - start
+    taken = jnp.where((ahead >= 0) & (ahead < count), 1.0, 0.0).astype(jnp.bfloat16)
+    line = lax.broadcasted_iota(jnp.int32, (16, blocks), 0)
+    facts = jnp.where(line == 0, lax.broadcasted_iota(jnp.int32, (16, blocks), 1), 1)
+    for at, fact in enumerate((rank, source, position, tile_at)):
+        facts = jnp.where(line == at + 1, fact, facts)
+    placed = lax.dot_general(
+        facts.astype(jnp.float32).astype(jnp.bfloat16), taken, NT, preferred_element_type=jnp.float32
+    )
+    placed = placed.astype(jnp.int32)
+    where_at = lax.broadcasted_iota(jnp.int32, (1, groups * full), 1) % full
+    sub = jnp.where(placed[5:6] > 0, where_at - placed[4:5], 0)
+    table_rows = [
+        placed[0:1] * per_block + sub,
+        placed[0:1],
+        placed[2:3],
+        jnp.clip(placed[1:2] - TILE * sub, 0, TILE),
+        placed[3:4] * per_block + sub,
+        jnp.broadcast_to(over, (1, groups * full)),
+    ]
+    table_rows = jnp.concatenate(table_rows + table_rows[-1:] * 2, axis=0)
+    for g in range(groups):
+        meta_ref[g] = table_rows[:, g * full : (g + 1) * full]
+    to_scalars = pltpu.make_async_copy(meta_ref, meta, meta_sem)
+    to_scalars.start()
+
+    early[1].wait()
+    entries = [mix_ref[c, d : d + 1, :] for c in range(components) for d in range(components)]
+    entries = jnp.concatenate(entries + entries[:1] * (16 - len(entries)), axis=0)
+    for b in range(blocks):
+        weight_ref[b] = jnp.broadcast_to(entries[:, b : b + 1], (16, lanes))
+
+    early[0].wait()
+    for s in range(owned):
+        x_ref[s] = field_ref[:, s * size : (s + 1) * size]
+    to_scalars.wait()
+    for copy in v_loads:
+        copy.wait()
+    for copy in later + u_loads:
+        copy.start()
+
+    lane = lax.broadcasted_iota(jnp.int32, (1, lanes), 1)
+    in_tile = lane % TILE
+    tile_of = lane // TILE
+
+    def spread(values):
+        vector = values[0]
+        for i, value in enumerate(values[1:]):
+            vector = jnp.where(tile_of == i + 1, value, vector)
+        return vector
+
+    def coef_step(offset, start, unroll):
+        to = jnp.bitwise_xor(me, offset)
+
+        def entry(fact, u, i):
+            return meta[to, fact, (start + u) * tiles_in + i]
+
+        v = jnp.concatenate(
+            [
+                v_ref[jnp.clip(entry(0, u, i), 0, tiles - 1)]
+                for u in range(unroll)
+                for i in range(tiles_in)
+            ],
+            axis=0,
+        )
+        x = x_ref[...].reshape(owned * channels, size)
+        y = lax.dot_general(x, v, NT, preferred_element_type=jnp.float32)
+        for u in range(unroll):
+            here = y[:, u * lanes : (u + 1) * lanes]
+            chosen = spread([entry(2, u, i) for i in range(tiles_in)])
+            coef = here[:channels]
+            for s in range(1, owned):
+                coef = jnp.where(chosen == s, here[s * channels : (s + 1) * channels], coef)
+            coef = jnp.where(in_tile < spread([entry(3, u, i) for i in range(tiles_in)]), coef, 0.0)
+            weight = spread(
+                [weight_ref[jnp.clip(entry(1, u, i), 0, blocks - 1)] for i in range(tiles_in)]
+            )
+            weights = [
+                [weight[c * components + d : c * components + d + 1] for d in range(components)]
+                for c in range(components)
+            ]
+            mixed = mix_rows(
+                weights, [coef[d * vectors : (d + 1) * vectors] for d in range(components)]
+            )
+            for h in range(HALVES):
+                for c in range(components):
+                    sent[offset, h, start + u, c * strip : (c + 1) * strip, :] = mixed[c][
+                        h * strip : (h + 1) * strip
+                    ].astype(jnp.bfloat16)
+
+    def coef_chunk(offset, begin, length):
+        unroll = next(u for u in (4, 3, 2, 1) if length % u == 0)
+
+        def several(step, carry):
+            coef_step(offset, begin + step * unroll, unroll)
+            return carry
+
+        lax.fori_loop(0, length // unroll, several, 0)
+
+    def exchange(offset, h, c):
+        where = (h, pl.ds(*plan[c]))
+        return pltpu.make_async_remote_copy(
+            src_ref=sent.at[(offset,) + where],
+            dst_ref=got.at[(offset - 1,) + where],
+            send_sem=send_sem.at[h, offset - 1, c],
+            recv_sem=recv_sem.at[h, offset - 1, c],
+            device_id={"tgt": jnp.bitwise_xor(me, offset)},
+            device_id_type=MESH,
+        )
+
+    def over_offsets(action):
+        def step(t, carry):
+            action(groups - 1 - t)
+            return carry
+
+        lax.fori_loop(0, groups - 1, step, 0)
+
+    def table_copy(offset):
+        to = jnp.bitwise_xor(me, offset)
+        return pltpu.make_async_remote_copy(
+            src_ref=meta_ref.at[to],
+            dst_ref=table_got.at[offset - 1],
+            send_sem=table_send.at[offset - 1],
+            recv_sem=table_recv.at[offset - 1],
+            device_id={"tgt": to},
+            device_id_type=MESH,
+        )
+
+    def table_down(offset):
+        return pltpu.make_async_copy(
+            table_got.at[offset - 1], table.at[offset - 1], table_sem.at[offset - 1]
+        )
+
+    pl.semaphore_wait(barrier, groups + shards + pairing - 3)
+    over_offsets(lambda offset: table_copy(offset).start())
+    for c, (begin, length) in enumerate(plan):
+
+        def one(offset):
+            coef_chunk(offset, begin, length)
+            exchange(offset, 0, c).start()
+
+        over_offsets(one)
+    for h in range(1, HALVES):
+        for c in range(len(plan)):
+            over_offsets(lambda offset: exchange(offset, h, c).start())
+    coef_chunk(0, 0, whole)
+
+    def fetch(offset):
+        table_copy(offset).wait_recv()
+        table_down(offset).start()
+
+    over_offsets(fetch)
+    for copy in later:
+        copy.wait()
+    for n in range(near_ref.shape[0]):
+        y = lax.dot_general(
+            x_ref[near_src[n]], near_ref[n], NT, preferred_element_type=jnp.float32
+        )
+        weights = [[near_mix[c, n, d] for d in range(components)] for c in range(components)]
+        mixed = mix_rows(weights, [y[d * vectors : (d + 1) * vectors] for d in range(components)])
+        for h in range(HALVES):
+            for c in range(components):
+                near_out[h, n, c * strip : (c + 1) * strip, :] = mixed[c][
+                    h * strip : (h + 1) * strip
+                ]
+
+    def place_near(w, carry):
+        for h in range(HALVES):
+            value = jnp.where(near_tgt[0] == w, near_out[h, 0], 0.0)
+            for n in range(1, near_ref.shape[0]):
+                value = value + jnp.where(near_tgt[n] == w, near_out[h, n], 0.0)
+            acc[h, pl.ds(pl.multiple_of(w * band, band), band), :] = value
+        return carry
+
+    lax.fori_loop(0, targets, place_near, 0)
+    for copy in u_loads:
+        copy.wait()
+
+    wide_tile = lax.broadcasted_iota(jnp.int32, (strip, lanes), 1) // TILE
+
+    def far(h, sender, entry, begin, length, read):
+        for u in range(length):
+            ids = None
+            for i in range(tiles_in):
+                at = jnp.clip(entry((begin + u) * tiles_in + i), 0, full - 1)
+                rhs[u * lanes + i * TILE : u * lanes + (i + 1) * TILE, :] = u_ref[sender * full + at]
+                target = cluster[sender * capacity + lax.div(at, per_block)]
+                ids = jnp.full((strip, lanes), target) if i == 0 else jnp.where(wide_tile == i, target, ids)
+            value = read(begin + u)
+            for w in range(targets):
+                on = jnp.where(ids == w, 1.0, 0.0).astype(jnp.bfloat16)
+                for c3 in range(components):
+                    lhs[pl.ds(w * band + c3 * strip, strip), u * lanes : (u + 1) * lanes] = (
+                        value[c3 * strip : (c3 + 1) * strip] * on
+                    )
+        acc[h] += jnp.dot(
+            lhs[:, : length * lanes], rhs[: length * lanes], preferred_element_type=jnp.float32
+        )
+
+    def far_own(h):
+        block = 8 if whole % 8 == 0 else 1
+
+        def several(c, carry):
+            far(h, me, lambda t: meta[me, 4, t], c * block, block, lambda m: sent[0, h, m])
+            return carry
+
+        lax.fori_loop(0, whole // block, several, 0)
+
+    def far_chunk(h, c):
+        def one(offset):
+            exchange(offset, h, c).wait_recv()
+            far(
+                h,
+                jnp.bitwise_xor(me, offset),
+                lambda t: table[offset - 1, 4, t],
+                *plan[c],
+                lambda m: got[offset - 1, h, m],
+            )
+
+        over_offsets(one)
+
+    def flag_copy(step):
+        axis, place, span, by = (
+            ("comp", half_of, pairing, step) if step < pairing else ("src", row, shards, step - pairing + 1)
+        )
+        kind = 0 if axis == "comp" else 1
+        return pltpu.make_async_remote_copy(
+            src_ref=flag_row.at[kind],
+            dst_ref=flag_got.at[step - 1],
+            send_sem=flag_send.at[step - 1],
+            recv_sem=flag_recv.at[step - 1],
+            device_id={axis: lax.rem(place + by, span)},
+            device_id_type=MESH,
+        )
+
+    comp_steps = range(1, pairing)
+    src_steps = range(pairing, pairing + shards - 1)
+
+    portion = shards * kept * band
+
+    def comp_copy(h, step):
+        to = lax.rem(half_of + step, pairing)
+        return pltpu.make_async_remote_copy(
+            src_ref=acc.at[h, pl.ds(pl.multiple_of(to * portion, portion), portion)],
+            dst_ref=comp_got.at[h, step - 1],
+            send_sem=comp_send.at[h, step - 1],
+            recv_sem=comp_recv.at[h, step - 1],
+            device_id={"comp": to},
+            device_id_type=MESH,
+        )
+
+    piece = kept * band
+
+    def src_copy(h, step):
+        to = lax.rem(row + step, shards)
+        return pltpu.make_async_remote_copy(
+            src_ref=cast.at[h, pl.ds(pl.multiple_of(to * piece, piece), piece)],
+            dst_ref=src_got.at[h, step - 1],
+            send_sem=src_send.at[h, step - 1],
+            recv_sem=src_recv.at[h, step - 1],
+            device_id={"src": to},
+            device_id_type=MESH,
+        )
+
+    def share_comp(h):
+        for step in range(1, pairing):
+            comp_copy(h, step).start()
+
+    def share_src(h):
+        for step in range(1, pairing):
+            comp_copy(h, step).wait_recv()
+        value = acc[h, pl.ds(pl.multiple_of(half_of * portion, portion), portion), :]
+        for step in range(1, pairing):
+            value = value + comp_got[h, step - 1]
+        total[h] = value
+        cast[h] = value.astype(jnp.bfloat16)
+        for step in range(1, shards):
+            src_copy(h, step).start()
+
+    def finish(h):
+        value = total[h, pl.ds(pl.multiple_of(row * piece, piece), piece), :]
+        for step in range(1, shards):
+            src_copy(h, step).wait_recv()
+            value = value + src_got[h, step - 1].astype(jnp.float32)
+        for k in range(kept):
+            for c in range(components):
+                at = k * band + c * strip
+                out_ref[c, h * strip : (h + 1) * strip, k * size : (k + 1) * size] = value[
+                    at : at + strip
+                ]
+
+    seen = over
+    for offset in range(1, groups):
+        seen = jnp.maximum(seen, table_got[offset - 1, 5:6, 0:1])
+        table_down(offset).wait()
+    flag_row[0] = jnp.broadcast_to(seen, flag_row.shape[1:])
+    for step in comp_steps:
+        flag_copy(step).start()
+    far_own(0)
+    seen = flag_row[0]
+    for step in comp_steps:
+        flag_copy(step).wait_recv()
+        seen = jnp.maximum(seen, flag_got[step - 1])
+    flag_row[1] = seen
+    for step in src_steps:
+        flag_copy(step).start()
+    for h in range(1, HALVES):
+        far_own(h)
+    seen = flag_row[1]
+    for step in src_steps:
+        flag_copy(step).wait_recv()
+        seen = jnp.maximum(seen, flag_got[step - 1])
+    flag_ref[...] = seen
+    for h in range(HALVES):
+        for c in range(len(plan)):
+            far_chunk(h, c)
+        share_comp(h)
+        share_src(h)
+        if h:
+            finish(h - 1)
+    finish(HALVES - 1)
+
+    over_offsets(lambda offset: table_copy(offset).wait_send())
+    for step in list(comp_steps) + list(src_steps):
+        flag_copy(step).wait_send()
+    for h in range(HALVES):
+        for c in range(len(plan)):
+            over_offsets(lambda offset: exchange(offset, h, c).wait_send())
         for step in range(1, pairing):
             comp_copy(h, step).wait_send()
         for step in range(1, shards):
@@ -385,63 +892,134 @@
     targets = owned * shards
     kept = targets // (pairing * shards)
     lanes = 2 * rank_width
-    chunk = 8 if pairs % 8 == 0 else pairs
-    chunks = pairs // chunk
     band = channels // HALVES
     near_count = near_matrix.shape[0]
-    smem = pl.BlockSpec(memory_space=pltpu.SMEM)
-    anywhere = pl.BlockSpec(memory_space=pl.ANY)
+    portion = shards * kept * band
     f32, bf16, i32 = jnp.float32, jnp.bfloat16, jnp.int32
     dma = pltpu.SemaphoreType.DMA
-    return pl.pallas_call(
-        functools.partial(fused_kernel, (groups, shards, pairing, components, chunk)),
-        out_shape=jax.ShapeDtypeStruct((components, vectors, kept * size), f32),
-        in_specs=[anywhere] * 4 + [smem] + [anywhere] * 2 + [smem] * 4 + [anywhere],
-        out_specs=pl.BlockSpec(memory_space=pltpu.VMEM),
-        scratch_shapes=[
-            pltpu.VMEM((channels, points), bf16),
-            pltpu.VMEM((owned, channels, size), bf16),
-            pltpu.VMEM((blocks, rank_width, size), bf16),
-            pltpu.VMEM((slots // 2, lanes, size), bf16),
-            pltpu.VMEM((near_count, size, size), bf16),
-            pltpu.VMEM((3, 1, blocks), i32),
-            pltpu.VMEM((8, slots), i32),
-            pltpu.SMEM((8, slots), i32),
-            pltpu.VMEM((HALVES, near_count, band, size), f32),
-            pltpu.VMEM((groups, HALVES, pairs, band, lanes), bf16),
-            pltpu.VMEM((groups - 1, HALVES, pairs, band, lanes), bf16),
-            pltpu.VMEM((targets * band, chunk * lanes), bf16),
-            pltpu.VMEM((HALVES, targets * band, size), f32),
-            pltpu.VMEM((HALVES, pairing - 1, shards * kept * band, size), f32),
-            pltpu.VMEM((HALVES, shards * kept * band, size), f32),
-            pltpu.VMEM((HALVES, shards * kept * band, size), bf16),
-            pltpu.VMEM((HALVES, shards - 1, kept * band, size), bf16),
-            dma((9,)),
-            dma((groups,)),
-            dma,
-            dma((HALVES, groups - 1, chunks)),
-            dma((HALVES, groups - 1, chunks)),
-            dma((HALVES, pairing - 1)),
-            dma((HALVES, pairing - 1)),
-            dma((HALVES, shards - 1)),
-            dma((HALVES, shards - 1)),
-        ],
-        compiler_params=pltpu.CompilerParams(collective_id=0, has_side_effects=True),
-        name="fused",
-    )(
+    result = pltpu.VMEM((components, vectors, kept * size), f32)
+    inputs = (
         field.reshape(channels, points),
         dest_group.reshape(1, -1),
         src_local.reshape(1, -1),
         ranks.reshape(1, -1),
         mixing.transpose(1, 2, 0),
-        v_factor,
-        u_factor.reshape(slots // 2, lanes, size),
+    )
+    near_inputs = (
         slot_cluster,
         near_src,
         near_tgt,
         near_mixing.transpose(1, 0, 2),
         near_matrix,
     )
+    near_scalars = [
+        pltpu.SMEM((slots,), i32),
+        pltpu.SMEM((near_count,), i32),
+        pltpu.SMEM((near_count,), i32),
+        pltpu.SMEM((components, near_count, components), f32),
+        pltpu.VMEM((HALVES, near_count, band, size), f32),
+    ]
+    reduce_buffers = [
+        pltpu.VMEM((HALVES, targets * band, size), f32),
+        pltpu.VMEM((HALVES, pairing - 1, portion, size), f32),
+        pltpu.VMEM((HALVES, portion, size), f32),
+        pltpu.VMEM((HALVES, portion, size), bf16),
+        pltpu.VMEM((HALVES, shards - 1, kept * band, size), bf16),
+        dma((14,)),
+        dma((groups,)),
+        dma,
+    ]
+    reduce_sems = [
+        dma((HALVES, pairing - 1)),
+        dma((HALVES, pairing - 1)),
+        dma((HALVES, shards - 1)),
+        dma((HALVES, shards - 1)),
+    ]
+    field_buffers = [
+        pltpu.VMEM((channels, points), bf16),
+        pltpu.VMEM((owned, channels, size), bf16),
+    ]
+
+    def padded():
+        chunk = 8 if pairs % 8 == 0 else pairs
+        return pl.pallas_call(
+            functools.partial(fused_kernel, (groups, shards, pairing, components, chunk)),
+            out_shape=result,
+            in_specs=[pl.BlockSpec(memory_space=pl.ANY)] * 12,
+            out_specs=pl.BlockSpec(memory_space=pltpu.VMEM),
+            scratch_shapes=field_buffers
+            + [
+                pltpu.VMEM((blocks, rank_width, size), bf16),
+                pltpu.VMEM((slots // 2, lanes, size), bf16),
+                pltpu.VMEM((near_count, size, size), bf16),
+                pltpu.VMEM((3, 1, blocks), i32),
+                pltpu.VMEM((8, slots), i32),
+                pltpu.SMEM((8, slots), i32),
+                pltpu.SMEM((components, components, blocks), f32),
+            ]
+            + near_scalars
+            + [
+                pltpu.VMEM((groups, HALVES, pairs, band, lanes), bf16),
+                pltpu.VMEM((groups - 1, HALVES, pairs, band, lanes), bf16),
+                pltpu.VMEM((targets * band, chunk * lanes), bf16),
+            ]
+            + reduce_buffers
+            + [dma((HALVES, groups - 1, pairs // chunk))] * 2
+            + reduce_sems,
+            compiler_params=pltpu.CompilerParams(collective_id=1, has_side_effects=True),
+            name="padded",
+        )(*inputs, v_factor, u_factor.reshape(slots // 2, lanes, size), *near_inputs)
+
+    per_block = rank_width // TILE
+    tiles_in = lanes // TILE
+    full = slots // groups * per_block
+    whole = full // tiles_in
+    share = 0.68 + (slots // groups) ** -0.5
+    limit = min(whole, math.ceil(whole * share))
+    plan = cut(limit)
+    value, flag = pl.pallas_call(
+        functools.partial(packed_kernel, (groups, shards, pairing, components, limit, plan)),
+        out_shape=(result, pltpu.VMEM((8, lanes), i32)),
+        in_specs=[pl.BlockSpec(memory_space=pl.ANY)] * 12,
+        out_specs=(pl.BlockSpec(memory_space=pltpu.VMEM),) * 2,
+        scratch_shapes=field_buffers
+        + [
+            pltpu.VMEM((blocks * per_block, TILE, size), bf16),
+            pltpu.VMEM((slots * per_block, TILE, size), bf16),
+            pltpu.VMEM((near_count, size, size), bf16),
+            pltpu.VMEM((3, 1, blocks), i32),
+            pltpu.VMEM((groups, 8, full), i32),
+            pltpu.SMEM((groups, 8, full), i32),
+            pltpu.VMEM((components, components, blocks), f32),
+            pltpu.VMEM((blocks, 16, lanes), f32),
+            pltpu.VMEM((groups - 1, 8, full), i32),
+            pltpu.SMEM((groups - 1, 8, full), i32),
+            pltpu.VMEM((2, 8, lanes), i32),
+            pltpu.VMEM((pairing + shards - 2, 8, lanes), i32),
+        ]
+        + near_scalars
+        + [
+            pltpu.VMEM((groups, HALVES, whole, band, lanes), bf16),
+            pltpu.VMEM((groups - 1, HALVES, limit, band, lanes), bf16),
+            pltpu.VMEM((targets * band, 8 * lanes), bf16),
+            pltpu.VMEM((8 * lanes, size), bf16),
+        ]
+        + reduce_buffers
+        + [dma((HALVES, groups - 1, len(plan)))] * 2
+        + reduce_sems
+        + [dma((groups - 1,))] * 3
+        + [dma((pairing + shards - 2,))] * 2,
+        compiler_params=pltpu.CompilerParams(collective_id=0, has_side_effects=True),
+        name="packed",
+    )(
+        *inputs,
+        v_factor.reshape(blocks * per_block, TILE, size),
+        u_factor.reshape(slots * per_block, TILE, size),
+        *near_inputs,
+    )
+    if limit == whole:
+        return value
+    return lax.cond(flag[0, 0] > 0, padded, lambda: value)
 
 
 def solution(mesh):

time: 53.2 us -> 45 us (0.85)
  Pallas kernels: 51.5 us -> 42.9 us
  between operations: 0.01 us -> 0.79 us
    pallas_call x1, Pallas kernels: 51.5 us -> 42.9 us  [body(): pl.pallas_call(functools.partial(packed_kernel, (groups, shards, pairing,...]
    unnamed x1 -> x21, local copies, waits for them, and re-layouts: 1.54 us -> 0.68 us
where the time goes in v1:
time: 45 us; the launch traced here: 44.9 us
  Pallas kernels  42.9 us (95%)
  local copies, waits for them, and re-layouts  1.2 us (3%)
  between operations  0.79 us (2%)
    pallas_call x1, Pallas kernels, body(): pl.pallas_call(functools.partial(packed_kernel, (groups, shards, pairing,...  42.9 us

profile of v1, /device:TPU:0, one launch (start us, length us, event | category | flops | bytes accessed | tf_op | source)
XLA Modules:
  0.0 44.9 jit_solution(10690186949583304750)
XLA Ops:
  0.0 0.0 copy-start
  0.0 0.0 copy-start.9
  0.0 0.0 copy-start.8
  0.0 0.0 copy-start.4
  0.0 0.0 copy-start.3
  0.0 0.0 copy-start.2
  0.0 0.0 copy-start.7
  0.0 0.0 copy-start.6
  0.0 0.0 copy-start.5
  0.1 0.0 copy-start.1
  0.1 42.9 %packed.1 = (f32[3,32,256]{2,1,0:T(8,128)S(1)}, s32[8,128]{1,0:T(8,128)S(1)}) custom-call(bf16[96,512]{1,0:T(8,128)(2,1)} %bitcast.13, s32[1,128]{1,0:T(1,128)} %bitcast.19, s32[1,128]{1,0:T(1,128)} %bitcast.21, s32[1,128]{1,0:T(1,128)} %bitcast.23, f32[3,3,128]{2,1,0:T(4,128)} %bitcast.15, bf16[512,16,256]{2,1,0:T(8,128)(2,1)} %bitcast.12, ...), custom_call_target="tpu_custom_call" | custom-call | tf_op jit(solution)/shard_map/packed/pallas_call | solution.py:980
  43.0 0.5 %slice.3 = s32[1,1]{1,0:T(1,128)} slice(s32[8,128]{1,0:T(8,128)S(1)} %get-tuple-element.47), slice={[0:1], [0:1]} | slice | bytes 8 | tf_op jit(solution)/shard_map/slice | solution.py:1022
  44.1 0.0 copy-done
  44.1 0.0 copy-done.9
  44.2 0.0 copy-done.8
  44.2 0.0 copy-done.4
  44.2 0.0 copy-done.3
  44.2 0.0 copy-done.2
  44.2 0.0 copy-done.7
  44.2 0.0 copy-done.6
  44.2 0.0 copy-done.5
  44.2 0.0 copy-done.1
  44.2 0.6 %copy.18 = f32[3,32,256]{2,1,0:T(8,128)} copy(f32[3,32,256]{2,1,0:T(8,128)S(1)} %get-tuple-element.49) | data formatting | bytes 196608
  (1 shorter events, 0.0 us)
Async XLA Ops:
  0.0 44.1 %copy-start = (bf16[4,256,256]{2,1,0:T(8,128)(2,1)S(1)}, bf16[4,256,256]{2,1,0:T(8,128)(2,1)}, u32[]{:S(2)}) copy-start(bf16[4,256,256]{2,1,0:T(8,128)(2,1)} %near_hbm.1) | copy-start | bytes 1572868
  0.0 44.1 %copy-start.9 = (s32[4]{0:T(128)S(1)}, s32[4]{0:T(128)}, u32[]{:S(2)}) copy-start(s32[4]{0:T(128)} %near_tgt_hbm.1) | copy-start | bytes 52
  0.0 44.2 %copy-start.8 = (s32[4]{0:T(128)S(1)}, s32[4]{0:T(128)}, u32[]{:S(2)}) copy-start(s32[4]{0:T(128)} %near_src_hbm.1) | copy-start | bytes 52
  0.0 44.2 %copy-start.4 = (s32[256]{0:T(256)S(1)}, s32[256]{0:T(256)}, u32[]{:S(2)}) copy-start(s32[256]{0:T(256)} %cluster_hbm.1) | copy-start | bytes 3076
  0.0 44.2 %copy-start.3 = (f32[4,3,3]{2,0,1:T(4,128)S(1)}, f32[4,3,3]{2,0,1:T(4,128)}, u32[]{:S(2)}) copy-start(f32[4,3,3]{2,0,1:T(4,128)} %param.24) | copy-start | bytes 436
  0.0 44.2 %copy-start.2 = (f32[128,3,3]{0,2,1:T(4,128)S(1)}, f32[128,3,3]{0,2,1:T(4,128)}, u32[]{:S(2)}) copy-start(f32[128,3,3]{0,2,1:T(4,128)} %param.18) | copy-start | bytes 13828
  0.0 44.2 %copy-start.7 = (s32[128]{0:T(128)S(1)}, s32[128]{0:T(128)}, u32[]{:S(2)}) copy-start(s32[128]{0:T(128)} %param.17) | copy-start | bytes 1540
  0.0 44.2 %copy-start.6 = (s32[128]{0:T(128)S(1)}, s32[128]{0:T(128)}, u32[]{:S(2)}) copy-start(s32[128]{0:T(128)} %param.16) | copy-start | bytes 1540
  0.0 44.2 %copy-start.5 = (s32[128,1]{0,1:T(1,128)S(1)}, s32[128,1]{0,1:T(1,128)}, u32[]{:S(2)}) copy-start(s32[128,1]{0,1:T(1,128)} %param.15) | copy-start | bytes 1540
  0.1 44.2 %copy-start.1 = (bf16[3,32,512]{2,1,0:T(8,128)(2,1)S(1)}, bf16[3,32,512]{2,1,0:T(8,128)(2,1)}, u32[]{:S(2)}) copy-start(bf16[3,32,512]{2,1,0:T(8,128)(2,1)} %param.14) | copy-start | bytes 294916

commit v2 on v1

--- a/solution.py
+++ b/solution.py
@@ -16,12 +16,16 @@
 
 
 def cut(length):
+    if length <= 8:
+        return ((0, length),)
     plan, begin = [], 0
-    while begin < length:
-        left = length - begin
-        size = 8 if left > 12 else min(left, max(4, left - 4))
-        plan.append((begin, size))
-        begin += size
+    while length - begin > 9:
+        plan.append((begin, 8))
+        begin += 8
+    most = (2 * (length - begin) + 2) // 3
+    plan.append((begin, most))
+    if length - begin > most:
+        plan.append((begin + most, length - begin - most))
     return tuple(plan)
 
 
@@ -712,46 +716,77 @@
 
     wide_tile = lax.broadcasted_iota(jnp.int32, (strip, lanes), 1) // TILE
 
-    def far(h, sender, entry, begin, length, read):
+    def build(n, sender, entry, begin, length, read):
         for u in range(length):
             ids = None
             for i in range(tiles_in):
                 at = jnp.clip(entry((begin + u) * tiles_in + i), 0, full - 1)
-                rhs[u * lanes + i * TILE : u * lanes + (i + 1) * TILE, :] = u_ref[sender * full + at]
+                rhs[n, u * lanes + i * TILE : u * lanes + (i + 1) * TILE, :] = u_ref[
+                    sender * full + at
+                ]
                 target = cluster[sender * capacity + lax.div(at, per_block)]
                 ids = jnp.full((strip, lanes), target) if i == 0 else jnp.where(wide_tile == i, target, ids)
             value = read(begin + u)
             for w in range(targets):
                 on = jnp.where(ids == w, 1.0, 0.0).astype(jnp.bfloat16)
                 for c3 in range(components):
-                    lhs[pl.ds(w * band + c3 * strip, strip), u * lanes : (u + 1) * lanes] = (
+                    lhs[n, pl.ds(w * band + c3 * strip, strip), u * lanes : (u + 1) * lanes] = (
                         value[c3 * strip : (c3 + 1) * strip] * on
                     )
+
+    def multiply(h, n, length):
         acc[h] += jnp.dot(
-            lhs[:, : length * lanes], rhs[: length * lanes], preferred_element_type=jnp.float32
-        )
+            lhs[n, :, : length * lanes], rhs[n, : length * lanes], preferred_element_type=jnp.float32
+        )
+
+    def far(h, work):
+        build(0, *work[0])
+        for n in range(1, len(work)):
+            build(n, *work[n])
+            multiply(h, n - 1, work[n - 1][3])
+        multiply(h, len(work) - 1, work[-1][3])
+
+    batch = 3 if (groups - 1) % 3 == 0 else 1
 
     def far_own(h):
         block = 8 if whole % 8 == 0 else 1
+        many = 2 if (whole // block) % 2 == 0 and batch > 1 else 1
 
         def several(c, carry):
-            far(h, me, lambda t: meta[me, 4, t], c * block, block, lambda m: sent[0, h, m])
-            return carry
-
-        lax.fori_loop(0, whole // block, several, 0)
-
-    def far_chunk(h, c):
-        def one(offset):
-            exchange(offset, h, c).wait_recv()
             far(
                 h,
-                jnp.bitwise_xor(me, offset),
-                lambda t: table[offset - 1, 4, t],
-                *plan[c],
-                lambda m: got[offset - 1, h, m],
+                [
+                    (me, lambda t: meta[me, 4, t], (c * many + n) * block, block, lambda m: sent[0, h, m])
+                    for n in range(many)
+                ],
             )
-
-        over_offsets(one)
+            return carry
+
+        lax.fori_loop(0, whole // block // many, several, 0)
+
+    def far_chunk(h, c):
+        def several(t, carry):
+            offsets = [groups - 1 - (t * batch + n) for n in range(batch)]
+            for offset in offsets:
+                exchange(offset, h, c).wait_recv()
+            far(
+                h,
+                [
+                    (
+                        jnp.bitwise_xor(me, offset),
+                        lambda t, offset=offset: table[offset - 1, 4, t],
+                        *plan[c],
+                        lambda m, offset=offset: got[offset - 1, h, m],
+                    )
+                    for offset in offsets
+                ],
+            )
+            return carry
+
+        if groups - 1 == batch:
+            several(0, 0)
+        else:
+            lax.fori_loop(0, (groups - 1) // batch, several, 0)
 
     def flag_copy(step):
         axis, place, span, by = (
@@ -772,21 +807,28 @@
 
     portion = shards * kept * band
 
-    def comp_copy(h, step):
+    piece = kept * band
+    power = shards & (shards - 1) == 0
+
+    def peer(step):
+        return jnp.bitwise_xor(row, step) if power else lax.rem(row + step, shards)
+
+    hops = list(range(shards - 1, -1, -1))
+
+    def comp_copy(h, step, hop):
         to = lax.rem(half_of + step, pairing)
+        which = pl.multiple_of(peer(hop) * piece, piece)
         return pltpu.make_async_remote_copy(
-            src_ref=acc.at[h, pl.ds(pl.multiple_of(to * portion, portion), portion)],
-            dst_ref=comp_got.at[h, step - 1],
-            send_sem=comp_send.at[h, step - 1],
-            recv_sem=comp_recv.at[h, step - 1],
+            src_ref=acc.at[h, pl.ds(pl.multiple_of(to * portion, portion) + which, piece)],
+            dst_ref=comp_got.at[h, step - 1, pl.ds(which, piece)],
+            send_sem=comp_send.at[h, step - 1, hop],
+            recv_sem=comp_recv.at[h, step - 1, hop],
             device_id={"comp": to},
             device_id_type=MESH,
         )
 
-    piece = kept * band
-
     def src_copy(h, step):
-        to = lax.rem(row + step, shards)
+        to = peer(step)
         return pltpu.make_async_remote_copy(
             src_ref=cast.at[h, pl.ds(pl.multiple_of(to * piece, piece), piece)],
             dst_ref=src_got.at[h, step - 1],
@@ -797,19 +839,23 @@
         )
 
     def share_comp(h):
-        for step in range(1, pairing):
-            comp_copy(h, step).start()
+        for hop in hops:
+            for step in range(1, pairing):
+                comp_copy(h, step, hop).start()
 
     def share_src(h):
-        for step in range(1, pairing):
-            comp_copy(h, step).wait_recv()
-        value = acc[h, pl.ds(pl.multiple_of(half_of * portion, portion), portion), :]
-        for step in range(1, pairing):
-            value = value + comp_got[h, step - 1]
-        total[h] = value
-        cast[h] = value.astype(jnp.bfloat16)
-        for step in range(1, shards):
-            src_copy(h, step).start()
+        mine = pl.multiple_of(half_of * portion, portion)
+        for hop in hops:
+            which = pl.multiple_of(peer(hop) * piece, piece)
+            value = acc[h, pl.ds(mine + which, piece), :]
+            for step in range(1, pairing):
+                comp_copy(h, step, hop).wait_recv()
+                value = value + comp_got[h, step - 1, pl.ds(which, piece), :]
+            if hop:
+                cast[h, pl.ds(which, piece), :] = value.astype(jnp.bfloat16)
+                src_copy(h, hop).start()
+            else:
+                total[h, pl.ds(which, piece), :] = value
 
     def finish(h):
         value = total[h, pl.ds(pl.multiple_of(row * piece, piece), piece), :]
@@ -861,7 +907,8 @@
         for c in range(len(plan)):
             over_offsets(lambda offset: exchange(offset, h, c).wait_send())
         for step in range(1, pairing):
-            comp_copy(h, step).wait_send()
+            for hop in hops:
+                comp_copy(h, step, hop).wait_send()
         for step in range(1, shards):
             src_copy(h, step).wait_send()
 
@@ -974,7 +1021,7 @@
     tiles_in = lanes // TILE
     full = slots // groups * per_block
     whole = full // tiles_in
-    share = 0.68 + (slots // groups) ** -0.5
+    share = 0.65 + (slots // groups) ** -0.5
     limit = min(whole, math.ceil(whole * share))
     plan = cut(limit)
     value, flag = pl.pallas_call(
@@ -1001,12 +1048,13 @@
         + [
             pltpu.VMEM((groups, HALVES, whole, band, lanes), bf16),
             pltpu.VMEM((groups - 1, HALVES, limit, band, lanes), bf16),
-            pltpu.VMEM((targets * band, 8 * lanes), bf16),
-            pltpu.VMEM((8 * lanes, size), bf16),
+            pltpu.VMEM((3, targets * band, 8 * lanes), bf16),
+            pltpu.VMEM((3, 8 * lanes, size), bf16),
         ]
         + reduce_buffers
         + [dma((HALVES, groups - 1, len(plan)))] * 2
-        + reduce_sems
+        + [dma((HALVES, pairing - 1, shards))] * 2
+        + reduce_sems[2:]
         + [dma((groups - 1,))] * 3
         + [dma((pairing + shards - 2,))] * 2,
         compiler_params=pltpu.CompilerParams(collective_id=0, has_side_effects=True),

time: 45 us -> 43.7 us (0.971)
  Pallas kernels: 42.9 us -> 41.5 us
    pallas_call x1, Pallas kernels: 42.9 us -> 41.5 us  [body(): pl.pallas_call(functools.partial(packed_kernel, (groups, shards, pairing,...]
where the time goes in v2:
time: 43.7 us; the launch traced here: 43.5 us
  Pallas kernels  41.5 us (95%)
  local copies, waits for them, and re-layouts  1.2 us (3%)
  between operations  0.8 us (2%)
    pallas_call x1, Pallas kernels, body(): pl.pallas_call(functools.partial(packed_kernel, (groups, shards, pairing,...  41.5 us

profile of v2, /device:TPU:0, one launch (start us, length us, event | category | flops | bytes accessed | tf_op | source)
XLA Modules:
  0.0 43.5 jit_solution(14928819699240783523)
XLA Ops:
  0.0 0.0 copy-start
  0.0 0.0 copy-start.9
  0.0 0.0 copy-start.8
  0.0 0.0 copy-start.4
  0.0 0.0 copy-start.3
  0.0 0.0 copy-start.2
  0.0 0.0 copy-start.7
  0.0 0.0 copy-start.6
  0.0 0.0 copy-start.5
  0.1 0.0 copy-start.1
  0.1 41.5 %packed.1 = (f32[3,32,256]{2,1,0:T(8,128)S(1)}, s32[8,128]{1,0:T(8,128)S(1)}) custom-call(bf16[96,512]{1,0:T(8,128)(2,1)} %bitcast.13, s32[1,128]{1,0:T(1,128)} %bitcast.19, s32[1,128]{1,0:T(1,128)} %bitcast.21, s32[1,128]{1,0:T(1,128)} %bitcast.23, f32[3,3,128]{2,1,0:T(4,128)} %bitcast.15, bf16[512,16,256]{2,1,0:T(8,128)(2,1)} %bitcast.12, ...), custom_call_target="tpu_custom_call" | custom-call | tf_op jit(solution)/shard_map/packed/pallas_call | solution.py:1027
  41.6 0.5 %slice.3 = s32[1,1]{1,0:T(1,128)} slice(s32[8,128]{1,0:T(8,128)S(1)} %get-tuple-element.47), slice={[0:1], [0:1]} | slice | bytes 8 | tf_op jit(solution)/shard_map/slice | solution.py:1070
  42.7 0.0 copy-done
  42.8 0.0 copy-done.9
  42.8 0.0 copy-done.8
  42.8 0.0 copy-done.4
  42.8 0.0 copy-done.3
  42.8 0.0 copy-done.2
  42.8 0.0 copy-done.7
  42.8 0.0 copy-done.6
  42.8 0.0 copy-done.5
  42.8 0.0 copy-done.1
  42.9 0.6 %copy.18 = f32[3,32,256]{2,1,0:T(8,128)} copy(f32[3,32,256]{2,1,0:T(8,128)S(1)} %get-tuple-element.49) | data formatting | bytes 196608
  (1 shorter events, 0.0 us)
Async XLA Ops:
  0.0 42.8 %copy-start = (bf16[4,256,256]{2,1,0:T(8,128)(2,1)S(1)}, bf16[4,256,256]{2,1,0:T(8,128)(2,1)}, u32[]{:S(2)}) copy-start(bf16[4,256,256]{2,1,0:T(8,128)(2,1)} %near_hbm.1) | copy-start | bytes 1572868
  0.0 42.8 %copy-start.9 = (s32[4]{0:T(128)S(1)}, s32[4]{0:T(128)}, u32[]{:S(2)}) copy-start(s32[4]{0:T(128)} %near_tgt_hbm.1) | copy-start | bytes 52
  0.0 42.8 %copy-start.8 = (s32[4]{0:T(128)S(1)}, s32[4]{0:T(128)}, u32[]{:S(2)}) copy-start(s32[4]{0:T(128)} %near_src_hbm.1) | copy-start | bytes 52
  0.0 42.8 %copy-start.4 = (s32[256]{0:T(256)S(1)}, s32[256]{0:T(256)}, u32[]{:S(2)}) copy-start(s32[256]{0:T(256)} %cluster_hbm.1) | copy-start | bytes 3076
  0.0 42.8 %copy-start.3 = (f32[4,3,3]{2,0,1:T(4,128)S(1)}, f32[4,3,3]{2,0,1:T(4,128)}, u32[]{:S(2)}) copy-start(f32[4,3,3]{2,0,1:T(4,128)} %param.24) | copy-start | bytes 436
  0.0 42.8 %copy-start.2 = (f32[128,3,3]{0,2,1:T(4,128)S(1)}, f32[128,3,3]{0,2,1:T(4,128)}, u32[]{:S(2)}) copy-start(f32[128,3,3]{0,2,1:T(4,128)} %param.18) | copy-start | bytes 13828
  0.0 42.8 %copy-start.7 = (s32[128]{0:T(128)S(1)}, s32[128]{0:T(128)}, u32[]{:S(2)}) copy-start(s32[128]{0:T(128)} %param.17) | copy-start | bytes 1540
  0.0 42.8 %copy-start.6 = (s32[128]{0:T(128)S(1)}, s32[128]{0:T(128)}, u32[]{:S(2)}) copy-start(s32[128]{0:T(128)} %param.16) | copy-start | bytes 1540
  0.0 42.8 %copy-start.5 = (s32[128,1]{0,1:T(1,128)S(1)}, s32[128,1]{0,1:T(1,128)}, u32[]{:S(2)}) copy-start(s32[128,1]{0,1:T(1,128)} %param.15) | copy-start | bytes 1540
  0.1 42.8 %copy-start.1 = (bf16[3,32,512]{2,1,0:T(8,128)(2,1)S(1)}, bf16[3,32,512]{2,1,0:T(8,128)(2,1)}, u32[]{:S(2)}) copy-start(bf16[3,32,512]{2,1,0:T(8,128)(2,1)} %param.14) | copy-start | bytes 294916
